TPU v7x, 256 devices: a whole 4x4x8 slice. The times are simulated.
256 devices in a mesh: tm: 16 (over z, core), space: 16 (over y, x).
Axes of the slice: x: 4, y: 4, z: 8, core: 2. Of those that a mesh axis runs over, the one named last changes fastest.
Arguments:
- residual: float32 [64, 32, 128, 128], P('tm', 'space'), may hold values from -6 to 6
- absorption: float32 [32, 128, 128], P('space'), may hold values from 0.05 to 1
- counts: int32 [64], replicated, may hold values from 1 to 6
Outputs:
- preconditioned: float32 [64, 32, 128, 128], P('tm', 'space')
Inputs may be any that keep to these rules, and one draw needn't show every extreme that they name: counts[k] is the number of minimal-residual steps of frequency k.
All inputs are finite; a program needn't handle non-finite values.
Results may differ from a plain program's by a relative error of at most 0.00022.
Values sent between devices are 32-bit elements; how exact they have to be, the bound alone decides.
No kernel may reach another device: no remote copies, remote signals or barrier semaphores. Data moves between devices by JAX's collectives and lax.ppermute only.
A program may use at most 64 MiB of HBM per device.

v0:
```python
import math
import jax
import jax.numpy as jnp
from jax import lax
from jax.sharding import PartitionSpec as P

L = 64
wrap_factor = 0.1
step_size = 1.0
norm_floor = 1e-06
highest = lax.Precision.HIGHEST


def with_halo(cells, sides, width):
    for axis, dim in sides:
        count = lax.axis_size(axis)
        ends = count - 1
        head = lax.slice_in_dim(cells, 0, width, axis=dim)
        tail = lax.slice_in_dim(cells, cells.shape[dim] - width, cells.shape[dim], axis=dim)
        cells = jnp.concatenate(
            [
                lax.ppermute(tail, axis, [(i, (i + 1) % count) for i in range(ends)]),
                cells,
                lax.ppermute(head, axis, [((i + 1) % count, i) for i in range(ends)]),
            ],
            axis=dim,
        )
    return cells


def copy_for_each(shard, axis):
    copies = jnp.broadcast_to(shard, (lax.axis_size(axis), *shard.shape))
    return lax.all_to_all(copies, axis, split_axis=0, concat_axis=0, tiled=True)


def taken_together(shard, axis):
    return copy_for_each(shard, axis).sum(axis=0)


def packed_total(arrays, axis):
    vector, at, finished = (jnp.concatenate([a.reshape(-1) for a in arrays]), 0, [])
    so_far = taken_together(vector, axis)
    for a in arrays:
        finished.append(so_far[at : at + a.size].reshape(a.shape))
        at += a.size
    return tuple(finished)


def shifts(frequency):
    angles = frequency.astype(jnp.float32) * (2.0 * math.pi / L)
    decay_rate = wrap_factor ** (1.0 / L)
    shift_re = (1.0 - decay_rate * jnp.cos(angles)) / step_size
    shift_im = decay_rate * jnp.sin(angles) / step_size
    return (shift_re, shift_im)


def near_sum(padded):
    interior = padded[..., 1:-1, :, :]
    widths = [(0, 0)] * (interior.ndim - 2) + [(1, 1), (1, 1)]
    padded_xy = jnp.pad(interior, widths)
    summed = padded[..., 2:, :, :] + padded[..., :-2, :, :]
    summed = summed + padded_xy[..., 2:, 1:-1] + padded_xy[..., :-2, 1:-1]
    summed = summed + padded_xy[..., 1:-1, 2:] + padded_xy[..., 1:-1, :-2]
    return summed


def advance(carried, dir_re, dir_im, img_re, img_im, coef_re, coef_im):
    sol_re, sol_im, res_re, res_im = carried
    sol_re = sol_re + coef_re * dir_re - coef_im * dir_im
    sol_im = sol_im + coef_re * dir_im + coef_im * dir_re
    res_re = res_re - (coef_re * img_re - coef_im * img_im)
    res_im = res_im - (coef_re * img_im + coef_im * img_re)
    return (sol_re, sol_im, res_re, res_im)


def solve_together(spectrum, absorption, frequencies, step_counts, longest):
    shift_re, shift_im = shifts(frequencies)
    shift_re = shift_re[:, None, None, None]
    shift_im = shift_im[:, None, None, None]
    diag_re = shift_re + 6.0 + absorption[None]
    magnitude = diag_re * diag_re + shift_im * shift_im
    inv_re = diag_re / magnitude
    inv_im = -shift_im / magnitude

    def iterate(iteration, carried):
        res_re, res_im = (carried[2], carried[3])
        dir_re = inv_re * res_re - inv_im * res_im
        dir_im = inv_re * res_im + inv_im * res_re
        padded = with_halo(jnp.stack([dir_re, dir_im], axis=1), (("space", 2),), 1)
        nearby = near_sum(padded)
        img_re = diag_re * dir_re - shift_im * dir_im - nearby[:, 0]
        img_im = diag_re * dir_im + shift_im * dir_re - nearby[:, 1]
        totals = packed_total(
            (
                jnp.sum(img_re * res_re + img_im * res_im, axis=(1, 2, 3)),
                jnp.sum(img_re * res_im - img_im * res_re, axis=(1, 2, 3)),
                jnp.sum(img_re * img_re + img_im * img_im, axis=(1, 2, 3)),
            ),
            "space",
        )
        active = iteration < step_counts
        denominator = totals[2] + norm_floor
        coef_re = jnp.where(active, totals[0] / denominator, 0.0)[:, None, None, None]
        coef_im = jnp.where(active, totals[1] / denominator, 0.0)[:, None, None, None]
        return advance(carried, dir_re, dir_im, img_re, img_im, coef_re, coef_im)

    blank = jnp.zeros_like(spectrum[:, 0])
    finished = lax.fori_loop(0, longest, iterate, (blank, blank, spectrum[:, 0], spectrum[:, 1]))
    return jnp.stack([finished[0], finished[1]], axis=1)


def slot_order():
    return jnp.arange(L, dtype=jnp.int32)


def phase_table(left, right):
    return (left[:, None] * right[None, :] % L).astype(jnp.float32) * (2.0 * math.pi / L)


def body(residual, absorption, counts):
    per_device = residual.shape[0]
    decay_rate = wrap_factor ** (1.0 / L)
    first_step = lax.axis_index("tm") * per_device
    times_here = first_step + jnp.arange(per_device, dtype=jnp.int32)
    scaled = residual * jnp.power(decay_rate, times_here.astype(jnp.float32))[:, None, None, None]
    slot_freqs = slot_order()
    own_freqs = lax.dynamic_slice_in_dim(slot_freqs, first_step, per_device)
    own_counts = counts[own_freqs]
    longest = jnp.max(counts)
    all_times = jnp.arange(L, dtype=jnp.int32)
    series = lax.all_to_all(scaled, "tm", split_axis=2, concat_axis=0, tiled=True)
    phases = phase_table(slot_freqs, all_times)
    real_part = jnp.einsum("sn,nzxy->szxy", jnp.cos(phases), series, precision=highest)
    imag_part = -jnp.einsum("sn,nzxy->szxy", jnp.sin(phases), series, precision=highest)
    spectrum = lax.all_to_all(
        jnp.stack([real_part, imag_part], axis=1), "tm", split_axis=0, concat_axis=3, tiled=True
    )
    solved = solve_together(spectrum, absorption, own_freqs, own_counts, longest)
    gathered = lax.all_to_all(solved, "tm", split_axis=3, concat_axis=0, tiled=True)
    phases = phase_table(all_times, slot_freqs)
    values = jnp.einsum("ns,szxy->nzxy", jnp.cos(phases), gathered[:, 0], precision=highest)
    values = values - jnp.einsum(
        "ns,szxy->nzxy", jnp.sin(phases), gathered[:, 1], precision=highest
    )
    weight = jnp.power(decay_rate, -all_times.astype(jnp.float32)) / L
    values = values * weight[:, None, None, None]
    return lax.all_to_all(values, "tm", split_axis=0, concat_axis=2, tiled=True)


def solution(mesh):
    in_specs = (P("tm", "space", None, None), P("space", None, None), P())
    out_specs = P("tm", "space", None, None)
    return jax.shard_map(body, mesh=mesh, in_specs=in_specs, out_specs=out_specs, check_vma=False)
```

profile of v0, /device:TPU:1, one launch (start us, length us, event | category | flops | bytes accessed | tf_op | source)
XLA Modules:
  0.0 341.6 jit_solution(1226429195683885706)
XLA Ops:
  1.5 27.0 %all_to_all.84 = f32[4,2,128,128]{3,0,1,2:T(4,128)S(1)} all-to-all(f32[4,2,128,128]{3,0,1,2:T(4,128)S(1)} %copy.60), channel_id=1, replica_groups=mesh['tm'=16,'space'=16] {'tm'}, dimensions={2} | all-to-all | bytes 1048576 | tf_op jit(solution)/shard_map/all_to_all | solution.py:131
  31.8 3.7 %all-to-all-start.2 = ((f32[64,2,2,8,128]{4,3,2,1,0:T(8,128)}), f32[64,2,2,8,128]{4,3,2,1,0:T(8,128)S(1)}, u32[]{:S(2)}, u32[]{:S(2)}) async-start(f32[64,2,2,8,128]{4,3,2,1,0:T(8,128)} %copy.62), calls=%async_computation.2 | async-start | bytes 2097152 | tf_op jit(solution)/shard_map/all_to_all | solution.py:135
  37.0 25.8 %all-to-all-done.2 = f32[64,2,2,8,128]{4,3,2,1,0:T(8,128)S(1)} async-done(((f32[64,2,2,8,128]{4,3,2,1,0:T(8,128)}), f32[64,2,2,8,128]{4,3,2,1,0:T(8,128)S(1)}, u32[]{:S(2)}, u32[]{:S(2)}) %all-to-all-start.2) | async-done | bytes 1048608 | tf_op jit(solution)/shard_map/all_to_all | solution.py:135
  64.7 204.2 %while.20 = (s32[]{:T(128)}, f32[4,2,128,128]{3,2,1,0:T(8,128)}, f32[4,2,128,128]{3,2,1,0:T(8,128)}, f32[4,2,128,128]{3,2,1,0:T(8,128)S(1)}, f32[4,2,128,128]{3,...) while((s32[]{:T(128)}, f32[4,2,128,128]{3,2,1,0:T(8,128)}, ...), condition=%wide.region_6.7_spmd.clone.clone, body=%wide.region_1.6_spmd.clone.clone.sunk | while | flops 9175258 | bytes 25447364 | solution.py:108
  65.8 3.2 collective-permute-start
  70.3 9.4 %collective-permute-done = f32[4,2,1,128,128]{4,3,2,0,1:T(8,128)S(1)} collective-permute-done((f32[4,2,1,128,128]{4,3,2,0,1:T(8,128)S(1)}, f32[4,2,1,128,128]{4,3,2,0,1:T(8,128)S(1)}, u32[]{:S(2)}, u32[]{:S(2)}) %collective-permute-start) | collective-permute-done | bytes 524320 | tf_op jit(solution)/shard_map/while/body/ppermute | solution.py:22
  79.8 4.1 %collective-permute-done.1 = f32[4,2,1,128,128]{4,3,2,0,1:T(8,128)S(1)} collective-permute-done((f32[4,2,1,128,128]{4,3,2,0,1:T(8,128)S(1)}, f32[4,2,1,128,128]{4,3,2,0,1:T(8,128)S(1)}, u32[]{:S(2)}, u32[]{:S(2)}) %collective-permute-start.1) | collective-permute-done | bytes 524320 | tf_op jit(solution)/shard_map/while/body/ppermute | solution.py:24
  85.9 8.3 %all-to-all-start = ((f32[16,1,12]{2,1,0:T(1,128)}), f32[16,1,12]{2,1,0:T(1,128)S(1)}, u32[]{:S(2)}, u32[]{:S(2)}) async-start(f32[16,1,12]{2,1,0:T(1,128)} %broadcast_in_dim.42), calls=%async_computation | async-start | bytes 16384 | tf_op jit(solution)/shard_map/while/body/all_to_all | solution.py:33
  94.2 6.4 %all-to-all-done = f32[16,1,12]{2,1,0:T(1,128)S(1)} async-done(((f32[16,1,12]{2,1,0:T(1,128)}), f32[16,1,12]{2,1,0:T(1,128)S(1)}, u32[]{:S(2)}, u32[]{:S(2)}) %all-to-all-start) | async-done | bytes 800 | tf_op jit(solution)/shard_map/while/body/all_to_all | solution.py:33
  108.1 8.1 %collective-permute-done = f32[4,2,1,128,128]{4,3,2,0,1:T(8,128)S(1)} collective-permute-done((f32[4,2,1,128,128]{4,3,2,0,1:T(8,128)S(1)}, f32[4,2,1,128,128]{4,3,2,0,1:T(8,128)S(1)}, u32[]{:S(2)}, u32[]{:S(2)}) %collective-permute-start) | collective-permute-done | bytes 524320 | tf_op jit(solution)/shard_map/while/body/ppermute | solution.py:22
  116.2 3.9 %collective-permute-done.1 = f32[4,2,1,128,128]{4,3,2,0,1:T(8,128)S(1)} collective-permute-done((f32[4,2,1,128,128]{4,3,2,0,1:T(8,128)S(1)}, f32[4,2,1,128,128]{4,3,2,0,1:T(8,128)S(1)}, u32[]{:S(2)}, u32[]{:S(2)}) %collective-permute-start.1) | collective-permute-done | bytes 524320 | tf_op jit(solution)/shard_map/while/body/ppermute | solution.py:24
  122.1 7.8 %all-to-all-start = ((f32[16,1,12]{2,1,0:T(1,128)}), f32[16,1,12]{2,1,0:T(1,128)S(1)}, u32[]{:S(2)}, u32[]{:S(2)}) async-start(f32[16,1,12]{2,1,0:T(1,128)} %broadcast_in_dim.42), calls=%async_computation | async-start | bytes 16384 | tf_op jit(solution)/shard_map/while/body/all_to_all | solution.py:33
  129.9 6.4 %all-to-all-done = f32[16,1,12]{2,1,0:T(1,128)S(1)} async-done(((f32[16,1,12]{2,1,0:T(1,128)}), f32[16,1,12]{2,1,0:T(1,128)S(1)}, u32[]{:S(2)}, u32[]{:S(2)}) %all-to-all-start) | async-done | bytes 800 | tf_op jit(solution)/shard_map/while/body/all_to_all | solution.py:33
  143.8 5.7 %collective-permute-done = f32[4,2,1,128,128]{4,3,2,0,1:T(8,128)S(1)} collective-permute-done((f32[4,2,1,128,128]{4,3,2,0,1:T(8,128)S(1)}, f32[4,2,1,128,128]{4,3,2,0,1:T(8,128)S(1)}, u32[]{:S(2)}, u32[]{:S(2)}) %collective-permute-start) | collective-permute-done | bytes 524320 | tf_op jit(solution)/shard_map/while/body/ppermute | solution.py:22
  149.5 3.9 %collective-permute-done.1 = f32[4,2,1,128,128]{4,3,2,0,1:T(8,128)S(1)} collective-permute-done((f32[4,2,1,128,128]{4,3,2,0,1:T(8,128)S(1)}, f32[4,2,1,128,128]{4,3,2,0,1:T(8,128)S(1)}, u32[]{:S(2)}, u32[]{:S(2)}) %collective-permute-start.1) | collective-permute-done | bytes 524320 | tf_op jit(solution)/shard_map/while/body/ppermute | solution.py:24
  155.3 7.8 %all-to-all-start = ((f32[16,1,12]{2,1,0:T(1,128)}), f32[16,1,12]{2,1,0:T(1,128)S(1)}, u32[]{:S(2)}, u32[]{:S(2)}) async-start(f32[16,1,12]{2,1,0:T(1,128)} %broadcast_in_dim.42), calls=%async_computation | async-start | bytes 16384 | tf_op jit(solution)/shard_map/while/body/all_to_all | solution.py:33
  163.2 6.4 %all-to-all-done = f32[16,1,12]{2,1,0:T(1,128)S(1)} async-done(((f32[16,1,12]{2,1,0:T(1,128)}), f32[16,1,12]{2,1,0:T(1,128)S(1)}, u32[]{:S(2)}, u32[]{:S(2)}) %all-to-all-start) | async-done | bytes 800 | tf_op jit(solution)/shard_map/while/body/all_to_all | solution.py:33
  177.0 4.7 %collective-permute-done = f32[4,2,1,128,128]{4,3,2,0,1:T(8,128)S(1)} collective-permute-done((f32[4,2,1,128,128]{4,3,2,0,1:T(8,128)S(1)}, f32[4,2,1,128,128]{4,3,2,0,1:T(8,128)S(1)}, u32[]{:S(2)}, u32[]{:S(2)}) %collective-permute-start) | collective-permute-done | bytes 524320 | tf_op jit(solution)/shard_map/while/body/ppermute | solution.py:22
  181.7 3.8 %collective-permute-done.1 = f32[4,2,1,128,128]{4,3,2,0,1:T(8,128)S(1)} collective-permute-done((f32[4,2,1,128,128]{4,3,2,0,1:T(8,128)S(1)}, f32[4,2,1,128,128]{4,3,2,0,1:T(8,128)S(1)}, u32[]{:S(2)}, u32[]{:S(2)}) %collective-permute-start.1) | collective-permute-done | bytes 524320 | tf_op jit(solution)/shard_map/while/body/ppermute | solution.py:24
  187.6 7.5 %all-to-all-start = ((f32[16,1,12]{2,1,0:T(1,128)}), f32[16,1,12]{2,1,0:T(1,128)S(1)}, u32[]{:S(2)}, u32[]{:S(2)}) async-start(f32[16,1,12]{2,1,0:T(1,128)} %broadcast_in_dim.42), calls=%async_computation | async-start | bytes 16384 | tf_op jit(solution)/shard_map/while/body/all_to_all | solution.py:33
  195.1 6.4 %all-to-all-done = f32[16,1,12]{2,1,0:T(1,128)S(1)} async-done(((f32[16,1,12]{2,1,0:T(1,128)}), f32[16,1,12]{2,1,0:T(1,128)S(1)}, u32[]{:S(2)}, u32[]{:S(2)}) %all-to-all-start) | async-done | bytes 800 | tf_op jit(solution)/shard_map/while/body/all_to_all | solution.py:33
  209.0 4.7 %collective-permute-done = f32[4,2,1,128,128]{4,3,2,0,1:T(8,128)S(1)} collective-permute-done((f32[4,2,1,128,128]{4,3,2,0,1:T(8,128)S(1)}, f32[4,2,1,128,128]{4,3,2,0,1:T(8,128)S(1)}, u32[]{:S(2)}, u32[]{:S(2)}) %collective-permute-start) | collective-permute-done | bytes 524320 | tf_op jit(solution)/shard_map/while/body/ppermute | solution.py:22
  213.6 3.8 %collective-permute-done.1 = f32[4,2,1,128,128]{4,3,2,0,1:T(8,128)S(1)} collective-permute-done((f32[4,2,1,128,128]{4,3,2,0,1:T(8,128)S(1)}, f32[4,2,1,128,128]{4,3,2,0,1:T(8,128)S(1)}, u32[]{:S(2)}, u32[]{:S(2)}) %collective-permute-start.1) | collective-permute-done | bytes 524320 | tf_op jit(solution)/shard_map/while/body/ppermute | solution.py:24
  219.5 7.5 %all-to-all-start = ((f32[16,1,12]{2,1,0:T(1,128)}), f32[16,1,12]{2,1,0:T(1,128)S(1)}, u32[]{:S(2)}, u32[]{:S(2)}) async-start(f32[16,1,12]{2,1,0:T(1,128)} %broadcast_in_dim.42), calls=%async_computation | async-start | bytes 16384 | tf_op jit(solution)/shard_map/while/body/all_to_all | solution.py:33
  227.0 6.4 %all-to-all-done = f32[16,1,12]{2,1,0:T(1,128)S(1)} async-done(((f32[16,1,12]{2,1,0:T(1,128)}), f32[16,1,12]{2,1,0:T(1,128)S(1)}, u32[]{:S(2)}, u32[]{:S(2)}) %all-to-all-start) | async-done | bytes 800 | tf_op jit(solution)/shard_map/while/body/all_to_all | solution.py:33
  240.9 4.7 %collective-permute-done = f32[4,2,1,128,128]{4,3,2,0,1:T(8,128)S(1)} collective-permute-done((f32[4,2,1,128,128]{4,3,2,0,1:T(8,128)S(1)}, f32[4,2,1,128,128]{4,3,2,0,1:T(8,128)S(1)}, u32[]{:S(2)}, u32[]{:S(2)}) %collective-permute-start) | collective-permute-done | bytes 524320 | tf_op jit(solution)/shard_map/while/body/ppermute | solution.py:22
  245.6 3.8 %collective-permute-done.1 = f32[4,2,1,128,128]{4,3,2,0,1:T(8,128)S(1)} collective-permute-done((f32[4,2,1,128,128]{4,3,2,0,1:T(8,128)S(1)}, f32[4,2,1,128,128]{4,3,2,0,1:T(8,128)S(1)}, u32[]{:S(2)}, u32[]{:S(2)}) %collective-permute-start.1) | collective-permute-done | bytes 524320 | tf_op jit(solution)/shard_map/while/body/ppermute | solution.py:24
  251.4 7.5 %all-to-all-start = ((f32[16,1,12]{2,1,0:T(1,128)}), f32[16,1,12]{2,1,0:T(1,128)S(1)}, u32[]{:S(2)}, u32[]{:S(2)}) async-start(f32[16,1,12]{2,1,0:T(1,128)} %broadcast_in_dim.42), calls=%async_computation | async-start | bytes 16384 | tf_op jit(solution)/shard_map/while/body/all_to_all | solution.py:33
  258.9 6.4 %all-to-all-done = f32[16,1,12]{2,1,0:T(1,128)S(1)} async-done(((f32[16,1,12]{2,1,0:T(1,128)}), f32[16,1,12]{2,1,0:T(1,128)S(1)}, u32[]{:S(2)}, u32[]{:S(2)}) %all-to-all-start) | async-done | bytes 800 | tf_op jit(solution)/shard_map/while/body/all_to_all | solution.py:33
  272.4 17.8 %all-to-all-start.3 = ((f32[4,2,2,128,128]{4,2,0,1,3:T(2,128)}), f32[4,2,2,128,128]{4,2,0,1,3:T(2,128)S(1)}, u32[]{:S(2)}, u32[]{:S(2)}) async-start(f32[4,2,2,128,128]{4,2,0,1,3:T(2,128)} %pad_maximum_fusion.7), calls=%async_computation.3 | async-start | bytes 2097152 | tf_op jit(solution)/shard_map/all_to_all | solution.py:139
  290.2 28.0 %all-to-all-done.3 = f32[4,2,2,128,128]{4,2,0,1,3:T(2,128)S(1)} async-done(((f32[4,2,2,128,128]{4,2,0,1,3:T(2,128)}), f32[4,2,2,128,128]{4,2,0,1,3:T(2,128)S(1)}, u32[]{:S(2)}, u32[]{:S(2)}) %all-to-all-start.3) | async-done | bytes 1048608 | tf_op jit(solution)/shard_map/all_to_all | solution.py:139
  320.3 20.4 %all_to_all.85 = f32[64,2,8,128]{3,2,1,0:T(8,128)S(1)} all-to-all(f32[64,2,8,128]{3,2,1,0:T(8,128)S(1)} %copy.67), channel_id=1, replica_groups=mesh['tm'=16,'space'=16] {'tm'}, dimensions={0} | all-to-all | bytes 1048576 | tf_op jit(solution)/shard_map/all_to_all | solution.py:147
  (102 shorter events, 64.6 us)
Async XLA Ops:
  31.8 3.9 %copy-start = (s32[64]{0:T(128)S(1)}, s32[64]{0:T(128)}, u32[]{:S(2)}) copy-start(s32[64]{0:T(128)} %param.7) | copy-start | bytes 772
  31.8 31.0 %all-to-all-start.2 = ((f32[64,2,2,8,128]{4,3,2,1,0:T(8,128)}), f32[64,2,2,8,128]{4,3,2,1,0:T(8,128)S(1)}, u32[]{:S(2)}, u32[]{:S(2)}) async-start(f32[64,2,2,8,128]{4,3,2,1,0:T(8,128)} %copy.62), calls=%async_computation.2 | async-start | bytes 2097152 | tf_op jit(solution)/shard_map/all_to_all | solution.py:135
  63.0 1.7 copy-start.1
  65.8 14.0 %collective-permute-start = (f32[4,2,1,128,128]{4,3,2,0,1:T(8,128)S(1)}, f32[4,2,1,128,128]{4,3,2,0,1:T(8,128)S(1)}, u32[]{:S(2)}, u32[]{:S(2)}) collective-permute-start(f32[4,2,1,128,128]{4,3,2,0,1:T(8,128)S(1)} %get-tuple-element.368), channel_id=1, source_target_pairs={{0,1},{1,2},{2,3},{3,4},{4,5},{5,6},{6,7},{7,8},{8,9},{9,10},{10,1... | collective-permute-start | bytes 1572872 | tf_op jit(solution)/shard_map/while/body/ppermute | solution.py:22
  68.9 15.0 %collective-permute-start.1 = (f32[4,2,1,128,128]{4,3,2,0,1:T(8,128)S(1)}, f32[4,2,1,128,128]{4,3,2,0,1:T(8,128)S(1)}, u32[]{:S(2)}, u32[]{:S(2)}) collective-permute-start(f32[4,2,1,128,128]{4,3,2,0,1:T(8,128)S(1)} %get-tuple-element.369), channel_id=1, source_target_pairs={{1,0},{2,1},{3,2},{4,3},{5,4},{6,5},{7,6},{8,7},{9,8},{10,9},{11,1... | collective-permute-start | bytes 1572872 | tf_op jit(solution)/shard_map/while/body/ppermute | solution.py:24
  85.9 14.7 %all-to-all-start = ((f32[16,1,12]{2,1,0:T(1,128)}), f32[16,1,12]{2,1,0:T(1,128)S(1)}, u32[]{:S(2)}, u32[]{:S(2)}) async-start(f32[16,1,12]{2,1,0:T(1,128)} %broadcast_in_dim.42), calls=%async_computation | async-start | bytes 16384 | tf_op jit(solution)/shard_map/while/body/all_to_all | solution.py:33
  104.6 11.6 %collective-permute-start = (f32[4,2,1,128,128]{4,3,2,0,1:T(8,128)S(1)}, f32[4,2,1,128,128]{4,3,2,0,1:T(8,128)S(1)}, u32[]{:S(2)}, u32[]{:S(2)}) collective-permute-start(f32[4,2,1,128,128]{4,3,2,0,1:T(8,128)S(1)} %get-tuple-element.368), channel_id=1, source_target_pairs={{0,1},{1,2},{2,3},{3,4},{4,5},{5,6},{6,7},{7,8},{8,9},{9,10},{10,1... | collective-permute-start | bytes 1572872 | tf_op jit(solution)/shard_map/while/body/ppermute | solution.py:22
  106.7 13.4 %collective-permute-start.1 = (f32[4,2,1,128,128]{4,3,2,0,1:T(8,128)S(1)}, f32[4,2,1,128,128]{4,3,2,0,1:T(8,128)S(1)}, u32[]{:S(2)}, u32[]{:S(2)}) collective-permute-start(f32[4,2,1,128,128]{4,3,2,0,1:T(8,128)S(1)} %get-tuple-element.369), channel_id=1, source_target_pairs={{1,0},{2,1},{3,2},{4,3},{5,4},{6,5},{7,6},{8,7},{9,8},{10,9},{11,1... | collective-permute-start | bytes 1572872 | tf_op jit(solution)/shard_map/while/body/ppermute | solution.py:24
  122.1 14.3 %all-to-all-start = ((f32[16,1,12]{2,1,0:T(1,128)}), f32[16,1,12]{2,1,0:T(1,128)S(1)}, u32[]{:S(2)}, u32[]{:S(2)}) async-start(f32[16,1,12]{2,1,0:T(1,128)} %broadcast_in_dim.42), calls=%async_computation | async-start | bytes 16384 | tf_op jit(solution)/shard_map/while/body/all_to_all | solution.py:33
  140.3 9.2 %collective-permute-start = (f32[4,2,1,128,128]{4,3,2,0,1:T(8,128)S(1)}, f32[4,2,1,128,128]{4,3,2,0,1:T(8,128)S(1)}, u32[]{:S(2)}, u32[]{:S(2)}) collective-permute-start(f32[4,2,1,128,128]{4,3,2,0,1:T(8,128)S(1)} %get-tuple-element.368), channel_id=1, source_target_pairs={{0,1},{1,2},{2,3},{3,4},{4,5},{5,6},{6,7},{7,8},{8,9},{9,10},{10,1... | collective-permute-start | bytes 1572872 | tf_op jit(solution)/shard_map/while/body/ppermute | solution.py:22
  142.4 11.0 %collective-permute-start.1 = (f32[4,2,1,128,128]{4,3,2,0,1:T(8,128)S(1)}, f32[4,2,1,128,128]{4,3,2,0,1:T(8,128)S(1)}, u32[]{:S(2)}, u32[]{:S(2)}) collective-permute-start(f32[4,2,1,128,128]{4,3,2,0,1:T(8,128)S(1)} %get-tuple-element.369), channel_id=1, source_target_pairs={{1,0},{2,1},{3,2},{4,3},{5,4},{6,5},{7,6},{8,7},{9,8},{10,9},{11,1... | collective-permute-start | bytes 1572872 | tf_op jit(solution)/shard_map/while/body/ppermute | solution.py:24
  155.3 14.3 %all-to-all-start = ((f32[16,1,12]{2,1,0:T(1,128)}), f32[16,1,12]{2,1,0:T(1,128)S(1)}, u32[]{:S(2)}, u32[]{:S(2)}) async-start(f32[16,1,12]{2,1,0:T(1,128)} %broadcast_in_dim.42), calls=%async_computation | async-start | bytes 16384 | tf_op jit(solution)/shard_map/while/body/all_to_all | solution.py:33
  173.6 8.2 %collective-permute-start = (f32[4,2,1,128,128]{4,3,2,0,1:T(8,128)S(1)}, f32[4,2,1,128,128]{4,3,2,0,1:T(8,128)S(1)}, u32[]{:S(2)}, u32[]{:S(2)}) collective-permute-start(f32[4,2,1,128,128]{4,3,2,0,1:T(8,128)S(1)} %get-tuple-element.368), channel_id=1, source_target_pairs={{0,1},{1,2},{2,3},{3,4},{4,5},{5,6},{6,7},{7,8},{8,9},{9,10},{10,1... | collective-permute-start | bytes 1572872 | tf_op jit(solution)/shard_map/while/body/ppermute | solution.py:22
  175.6 9.9 %collective-permute-start.1 = (f32[4,2,1,128,128]{4,3,2,0,1:T(8,128)S(1)}, f32[4,2,1,128,128]{4,3,2,0,1:T(8,128)S(1)}, u32[]{:S(2)}, u32[]{:S(2)}) collective-permute-start(f32[4,2,1,128,128]{4,3,2,0,1:T(8,128)S(1)} %get-tuple-element.369), channel_id=1, source_target_pairs={{1,0},{2,1},{3,2},{4,3},{5,4},{6,5},{7,6},{8,7},{9,8},{10,9},{11,1... | collective-permute-start | bytes 1572872 | tf_op jit(solution)/shard_map/while/body/ppermute | solution.py:24
  187.6 14.0 %all-to-all-start = ((f32[16,1,12]{2,1,0:T(1,128)}), f32[16,1,12]{2,1,0:T(1,128)S(1)}, u32[]{:S(2)}, u32[]{:S(2)}) async-start(f32[16,1,12]{2,1,0:T(1,128)} %broadcast_in_dim.42), calls=%async_computation | async-start | bytes 16384 | tf_op jit(solution)/shard_map/while/body/all_to_all | solution.py:33
  205.5 8.2 %collective-permute-start = (f32[4,2,1,128,128]{4,3,2,0,1:T(8,128)S(1)}, f32[4,2,1,128,128]{4,3,2,0,1:T(8,128)S(1)}, u32[]{:S(2)}, u32[]{:S(2)}) collective-permute-start(f32[4,2,1,128,128]{4,3,2,0,1:T(8,128)S(1)} %get-tuple-element.368), channel_id=1, source_target_pairs={{0,1},{1,2},{2,3},{3,4},{4,5},{5,6},{6,7},{7,8},{8,9},{9,10},{10,1... | collective-permute-start | bytes 1572872 | tf_op jit(solution)/shard_map/while/body/ppermute | solution.py:22
  207.6 9.9 %collective-permute-start.1 = (f32[4,2,1,128,128]{4,3,2,0,1:T(8,128)S(1)}, f32[4,2,1,128,128]{4,3,2,0,1:T(8,128)S(1)}, u32[]{:S(2)}, u32[]{:S(2)}) collective-permute-start(f32[4,2,1,128,128]{4,3,2,0,1:T(8,128)S(1)} %get-tuple-element.369), channel_id=1, source_target_pairs={{1,0},{2,1},{3,2},{4,3},{5,4},{6,5},{7,6},{8,7},{9,8},{10,9},{11,1... | collective-permute-start | bytes 1572872 | tf_op jit(solution)/shard_map/while/body/ppermute | solution.py:24
  219.5 14.0 %all-to-all-start = ((f32[16,1,12]{2,1,0:T(1,128)}), f32[16,1,12]{2,1,0:T(1,128)S(1)}, u32[]{:S(2)}, u32[]{:S(2)}) async-start(f32[16,1,12]{2,1,0:T(1,128)} %broadcast_in_dim.42), calls=%async_computation | async-start | bytes 16384 | tf_op jit(solution)/shard_map/while/body/all_to_all | solution.py:33
  237.4 8.2 %collective-permute-start = (f32[4,2,1,128,128]{4,3,2,0,1:T(8,128)S(1)}, f32[4,2,1,128,128]{4,3,2,0,1:T(8,128)S(1)}, u32[]{:S(2)}, u32[]{:S(2)}) collective-permute-start(f32[4,2,1,128,128]{4,3,2,0,1:T(8,128)S(1)} %get-tuple-element.368), channel_id=1, source_target_pairs={{0,1},{1,2},{2,3},{3,4},{4,5},{5,6},{6,7},{7,8},{8,9},{9,10},{10,1... | collective-permute-start | bytes 1572872 | tf_op jit(solution)/shard_map/while/body/ppermute | solution.py:22
  239.5 9.9 %collective-permute-start.1 = (f32[4,2,1,128,128]{4,3,2,0,1:T(8,128)S(1)}, f32[4,2,1,128,128]{4,3,2,0,1:T(8,128)S(1)}, u32[]{:S(2)}, u32[]{:S(2)}) collective-permute-start(f32[4,2,1,128,128]{4,3,2,0,1:T(8,128)S(1)} %get-tuple-element.369), channel_id=1, source_target_pairs={{1,0},{2,1},{3,2},{4,3},{5,4},{6,5},{7,6},{8,7},{9,8},{10,9},{11,1... | collective-permute-start | bytes 1572872 | tf_op jit(solution)/shard_map/while/body/ppermute | solution.py:24
  251.4 14.0 %all-to-all-start = ((f32[16,1,12]{2,1,0:T(1,128)}), f32[16,1,12]{2,1,0:T(1,128)S(1)}, u32[]{:S(2)}, u32[]{:S(2)}) async-start(f32[16,1,12]{2,1,0:T(1,128)} %broadcast_in_dim.42), calls=%async_computation | async-start | bytes 16384 | tf_op jit(solution)/shard_map/while/body/all_to_all | solution.py:33
  272.4 45.9 %all-to-all-start.3 = ((f32[4,2,2,128,128]{4,2,0,1,3:T(2,128)}), f32[4,2,2,128,128]{4,2,0,1,3:T(2,128)S(1)}, u32[]{:S(2)}, u32[]{:S(2)}) async-start(f32[4,2,2,128,128]{4,2,0,1,3:T(2,128)} %pad_maximum_fusion.7), calls=%async_computation.3 | async-start | bytes 2097152 | tf_op jit(solution)/shard_map/all_to_all | solution.py:139
where the time goes:
time: 343 us; the launch traced here: 342 us
  waiting for transfers between devices  153 us (45%)
  starting transfers between devices  89.2 us (26%)
  blocking collectives  47.4 us (14%)
  other arithmetic  32 us (9%)
  local copies, waits for them, and re-layouts  11.6 us (3%)
  loops' own time  5.21 us (2%)
    all_to_all x6, starting transfers between devices, copy_for_each(): return lax.all_to_all(copies, axis, split_axis=0, concat_axis=0, tiled=True)  46.4 us
    all_to_all x6, waiting for transfers between devices, copy_for_each(): return lax.all_to_all(copies, axis, split_axis=0, concat_axis=0, tiled=True)  38.6 us
    ppermute x6, waiting for transfers between devices, with_halo(): lax.ppermute(tail, axis, [(i, (i + 1) % count) for i in range(ends)])  37.3 us
    all_to_all x1, waiting for transfers between devices, body(): lax.all_to_all(solved, 'tm', split_axis=3, concat_axis=0, tiled=True)  28 us
    all_to_all x1, blocking collectives, body(): lax.all_to_all(scaled, 'tm', split_axis=2, concat_axis=0, tiled=True)  27 us
    all_to_all x1, waiting for transfers between devices, body(): lax.all_to_all(jnp.stack([real_part, imag_part], axis=1), 'tm', split_axi...  25.8 us
    ppermute x6, waiting for transfers between devices, with_halo(): lax.ppermute(head, axis, [((i + 1) % count, i) for i in range(ends)])  23.4 us
    all_to_all x1, blocking collectives, body(): return lax.all_to_all(values, 'tm', split_axis=0, concat_axis=2, tiled=True)  20.4 us
  transfers between devices with their start and end apart: 20, of which 20 were waited for; matrix products, arithmetic and copies ran while one was open for 1% of the time, Pallas kernels for 0%

commit v1 on v0

--- a/solution.py
+++ b/solution.py
@@ -132,9 +132,10 @@
     phases = phase_table(slot_freqs, all_times)
     real_part = jnp.einsum("sn,nzxy->szxy", jnp.cos(phases), series, precision=highest)
     imag_part = -jnp.einsum("sn,nzxy->szxy", jnp.sin(phases), series, precision=highest)
-    spectrum = lax.all_to_all(
-        jnp.stack([real_part, imag_part], axis=1), "tm", split_axis=0, concat_axis=3, tiled=True
-    )
+    block = jnp.stack([real_part, imag_part], axis=1)
+    pieces = jnp.split(block, lax.axis_size("tm"), axis=0)
+    arrived = lax.all_to_all(jnp.stack(pieces), "tm", 0, 0)
+    spectrum = jnp.concatenate(arrived, axis=3)
     solved = solve_together(spectrum, absorption, own_freqs, own_counts, longest)
     gathered = lax.all_to_all(solved, "tm", split_axis=3, concat_axis=0, tiled=True)
     phases = phase_table(all_times, slot_freqs)

time: 343 us -> 351 us (1.023)
  other arithmetic: 32 us -> 42.2 us
    unnamed x0 -> x15, other arithmetic: none -> 9.66 us
where the time goes in v1:
time: 351 us; the launch traced here: 350 us
  waiting for transfers between devices  153 us (44%)
  starting transfers between devices  89.2 us (25%)
  blocking collectives  47.4 us (14%)
  other arithmetic  42.2 us (12%)
  local copies, waits for them, and re-layouts  10 us (3%)
  loops' own time  5.21 us (1%)
    all_to_all x6, starting transfers between devices, copy_for_each(): return lax.all_to_all(copies, axis, split_axis=0, concat_axis=0, tiled=True)  46.4 us
    all_to_all x6, waiting for transfers between devices, copy_for_each(): return lax.all_to_all(copies, axis, split_axis=0, concat_axis=0, tiled=True)  38.6 us
    ppermute x6, waiting for transfers between devices, with_halo(): lax.ppermute(tail, axis, [(i, (i + 1) % count) for i in range(ends)])  37.3 us
    all_to_all x1, waiting for transfers between devices, body(): lax.all_to_all(solved, 'tm', split_axis=3, concat_axis=0, tiled=True)  28 us
    all_to_all x1, blocking collectives, body(): lax.all_to_all(scaled, 'tm', split_axis=2, concat_axis=0, tiled=True)  27 us
    all_to_all x1, waiting for transfers between devices, body(): arrived = lax.all_to_all(jnp.stack(pieces), 'tm', 0, 0)  25.8 us
    ppermute x6, waiting for transfers between devices, with_halo(): lax.ppermute(head, axis, [((i + 1) % count, i) for i in range(ends)])  23.4 us
    all_to_all x1, blocking collectives, body(): return lax.all_to_all(values, 'tm', split_axis=0, concat_axis=2, tiled=True)  20.4 us
  transfers between devices with their start and end apart: 20, of which 20 were waited for; matrix products, arithmetic and copies ran while one was open for 1% of the time, Pallas kernels for 0%

profile of v1, /device:TPU:1, one launch (start us, length us, event | category | flops | bytes accessed | tf_op | source)
XLA Modules:
  0.0 350.2 jit_solution(7412452106764786136)
XLA Ops:
  1.5 27.0 %all_to_all.71 = f32[4,2,128,128]{3,0,1,2:T(4,128)S(1)} all-to-all(f32[4,2,128,128]{3,0,1,2:T(4,128)S(1)} %copy.54), channel_id=1, replica_groups=mesh['tm'=16,'space'=16] {'tm'}, dimensions={2} | all-to-all | bytes 1048576 | tf_op jit(solution)/shard_map/all_to_all | solution.py:131
  40.4 3.7 %all-to-all-start.2 = ((f32[16,4,2,2,8,128]{5,1,4,3,2,0:T(4,128)}), f32[16,4,2,2,8,128]{5,1,4,3,2,0:T(4,128)S(1)}, u32[]{:S(2)}, u32[]{:S(2)}) async-start(f32[16,4,2,2,8,128]{5,1,4,3,2,0:T(4,128)} %fusion.38), calls=%async_computation.2 | async-start | bytes 2097152 | tf_op jit(solution)/shard_map/all_to_all | solution.py:137
  45.6 25.8 %all-to-all-done.2 = f32[16,4,2,2,8,128]{5,1,4,3,2,0:T(4,128)S(1)} async-done(((f32[16,4,2,2,8,128]{5,1,4,3,2,0:T(4,128)}), f32[16,4,2,2,8,128]{5,1,4,3,2,0:T(4,128)S(1)}, u32[]{:S(2)}, u32[]{:S(2)}) %all-to-all-start.2) | async-done | bytes 1048608 | tf_op jit(solution)/shard_map/all_to_all | solution.py:137
  73.3 204.2 %while.20 = (s32[]{:T(128)}, f32[4,2,128,128]{3,2,1,0:T(8,128)}, f32[4,2,128,128]{3,2,1,0:T(8,128)}, f32[4,2,128,128]{3,2,1,0:T(8,128)S(1)}, f32[4,2,128,128]{3,...) while((s32[]{:T(128)}, f32[4,2,128,128]{3,2,1,0:T(8,128)}, ...), condition=%wide.region_6.7_spmd.clone.clone, body=%wide.region_1.6_spmd.clone.clone.sunk | while | flops 9175258 | bytes 25447364 | solution.py:108
  74.4 3.1 collective-permute-start
  78.9 9.4 %collective-permute-done = f32[4,2,1,128,128]{4,3,2,0,1:T(8,128)S(1)} collective-permute-done((f32[4,2,1,128,128]{4,3,2,0,1:T(8,128)S(1)}, f32[4,2,1,128,128]{4,3,2,0,1:T(8,128)S(1)}, u32[]{:S(2)}, u32[]{:S(2)}) %collective-permute-start) | collective-permute-done | bytes 524320 | tf_op jit(solution)/shard_map/while/body/ppermute | solution.py:22
  88.4 4.1 %collective-permute-done.1 = f32[4,2,1,128,128]{4,3,2,0,1:T(8,128)S(1)} collective-permute-done((f32[4,2,1,128,128]{4,3,2,0,1:T(8,128)S(1)}, f32[4,2,1,128,128]{4,3,2,0,1:T(8,128)S(1)}, u32[]{:S(2)}, u32[]{:S(2)}) %collective-permute-start.1) | collective-permute-done | bytes 524320 | tf_op jit(solution)/shard_map/while/body/ppermute | solution.py:24
  94.5 8.3 %all-to-all-start = ((f32[16,1,12]{2,1,0:T(1,128)}), f32[16,1,12]{2,1,0:T(1,128)S(1)}, u32[]{:S(2)}, u32[]{:S(2)}) async-start(f32[16,1,12]{2,1,0:T(1,128)} %broadcast_in_dim.42), calls=%async_computation | async-start | bytes 16384 | tf_op jit(solution)/shard_map/while/body/all_to_all | solution.py:33
  102.8 6.4 %all-to-all-done = f32[16,1,12]{2,1,0:T(1,128)S(1)} async-done(((f32[16,1,12]{2,1,0:T(1,128)}), f32[16,1,12]{2,1,0:T(1,128)S(1)}, u32[]{:S(2)}, u32[]{:S(2)}) %all-to-all-start) | async-done | bytes 800 | tf_op jit(solution)/shard_map/while/body/all_to_all | solution.py:33
  116.7 8.1 %collective-permute-done = f32[4,2,1,128,128]{4,3,2,0,1:T(8,128)S(1)} collective-permute-done((f32[4,2,1,128,128]{4,3,2,0,1:T(8,128)S(1)}, f32[4,2,1,128,128]{4,3,2,0,1:T(8,128)S(1)}, u32[]{:S(2)}, u32[]{:S(2)}) %collective-permute-start) | collective-permute-done | bytes 524320 | tf_op jit(solution)/shard_map/while/body/ppermute | solution.py:22
  124.8 3.9 %collective-permute-done.1 = f32[4,2,1,128,128]{4,3,2,0,1:T(8,128)S(1)} collective-permute-done((f32[4,2,1,128,128]{4,3,2,0,1:T(8,128)S(1)}, f32[4,2,1,128,128]{4,3,2,0,1:T(8,128)S(1)}, u32[]{:S(2)}, u32[]{:S(2)}) %collective-permute-start.1) | collective-permute-done | bytes 524320 | tf_op jit(solution)/shard_map/while/body/ppermute | solution.py:24
  130.7 7.8 %all-to-all-start = ((f32[16,1,12]{2,1,0:T(1,128)}), f32[16,1,12]{2,1,0:T(1,128)S(1)}, u32[]{:S(2)}, u32[]{:S(2)}) async-start(f32[16,1,12]{2,1,0:T(1,128)} %broadcast_in_dim.42), calls=%async_computation | async-start | bytes 16384 | tf_op jit(solution)/shard_map/while/body/all_to_all | solution.py:33
  138.5 6.4 %all-to-all-done = f32[16,1,12]{2,1,0:T(1,128)S(1)} async-done(((f32[16,1,12]{2,1,0:T(1,128)}), f32[16,1,12]{2,1,0:T(1,128)S(1)}, u32[]{:S(2)}, u32[]{:S(2)}) %all-to-all-start) | async-done | bytes 800 | tf_op jit(solution)/shard_map/while/body/all_to_all | solution.py:33
  152.4 5.7 %collective-permute-done = f32[4,2,1,128,128]{4,3,2,0,1:T(8,128)S(1)} collective-permute-done((f32[4,2,1,128,128]{4,3,2,0,1:T(8,128)S(1)}, f32[4,2,1,128,128]{4,3,2,0,1:T(8,128)S(1)}, u32[]{:S(2)}, u32[]{:S(2)}) %collective-permute-start) | collective-permute-done | bytes 524320 | tf_op jit(solution)/shard_map/while/body/ppermute | solution.py:22
  158.1 3.9 %collective-permute-done.1 = f32[4,2,1,128,128]{4,3,2,0,1:T(8,128)S(1)} collective-permute-done((f32[4,2,1,128,128]{4,3,2,0,1:T(8,128)S(1)}, f32[4,2,1,128,128]{4,3,2,0,1:T(8,128)S(1)}, u32[]{:S(2)}, u32[]{:S(2)}) %collective-permute-start.1) | collective-permute-done | bytes 524320 | tf_op jit(solution)/shard_map/while/body/ppermute | solution.py:24
  164.0 7.8 %all-to-all-start = ((f32[16,1,12]{2,1,0:T(1,128)}), f32[16,1,12]{2,1,0:T(1,128)S(1)}, u32[]{:S(2)}, u32[]{:S(2)}) async-start(f32[16,1,12]{2,1,0:T(1,128)} %broadcast_in_dim.42), calls=%async_computation | async-start | bytes 16384 | tf_op jit(solution)/shard_map/while/body/all_to_all | solution.py:33
  171.8 6.4 %all-to-all-done = f32[16,1,12]{2,1,0:T(1,128)S(1)} async-done(((f32[16,1,12]{2,1,0:T(1,128)}), f32[16,1,12]{2,1,0:T(1,128)S(1)}, u32[]{:S(2)}, u32[]{:S(2)}) %all-to-all-start) | async-done | bytes 800 | tf_op jit(solution)/shard_map/while/body/all_to_all | solution.py:33
  185.7 4.7 %collective-permute-done = f32[4,2,1,128,128]{4,3,2,0,1:T(8,128)S(1)} collective-permute-done((f32[4,2,1,128,128]{4,3,2,0,1:T(8,128)S(1)}, f32[4,2,1,128,128]{4,3,2,0,1:T(8,128)S(1)}, u32[]{:S(2)}, u32[]{:S(2)}) %collective-permute-start) | collective-permute-done | bytes 524320 | tf_op jit(solution)/shard_map/while/body/ppermute | solution.py:22
  190.3 3.8 %collective-permute-done.1 = f32[4,2,1,128,128]{4,3,2,0,1:T(8,128)S(1)} collective-permute-done((f32[4,2,1,128,128]{4,3,2,0,1:T(8,128)S(1)}, f32[4,2,1,128,128]{4,3,2,0,1:T(8,128)S(1)}, u32[]{:S(2)}, u32[]{:S(2)}) %collective-permute-start.1) | collective-permute-done | bytes 524320 | tf_op jit(solution)/shard_map/while/body/ppermute | solution.py:24
  196.2 7.5 %all-to-all-start = ((f32[16,1,12]{2,1,0:T(1,128)}), f32[16,1,12]{2,1,0:T(1,128)S(1)}, u32[]{:S(2)}, u32[]{:S(2)}) async-start(f32[16,1,12]{2,1,0:T(1,128)} %broadcast_in_dim.42), calls=%async_computation | async-start | bytes 16384 | tf_op jit(solution)/shard_map/while/body/all_to_all | solution.py:33
  203.7 6.4 %all-to-all-done = f32[16,1,12]{2,1,0:T(1,128)S(1)} async-done(((f32[16,1,12]{2,1,0:T(1,128)}), f32[16,1,12]{2,1,0:T(1,128)S(1)}, u32[]{:S(2)}, u32[]{:S(2)}) %all-to-all-start) | async-done | bytes 800 | tf_op jit(solution)/shard_map/while/body/all_to_all | solution.py:33
  217.6 4.7 %collective-permute-done = f32[4,2,1,128,128]{4,3,2,0,1:T(8,128)S(1)} collective-permute-done((f32[4,2,1,128,128]{4,3,2,0,1:T(8,128)S(1)}, f32[4,2,1,128,128]{4,3,2,0,1:T(8,128)S(1)}, u32[]{:S(2)}, u32[]{:S(2)}) %collective-permute-start) | collective-permute-done | bytes 524320 | tf_op jit(solution)/shard_map/while/body/ppermute | solution.py:22
  222.3 3.8 %collective-permute-done.1 = f32[4,2,1,128,128]{4,3,2,0,1:T(8,128)S(1)} collective-permute-done((f32[4,2,1,128,128]{4,3,2,0,1:T(8,128)S(1)}, f32[4,2,1,128,128]{4,3,2,0,1:T(8,128)S(1)}, u32[]{:S(2)}, u32[]{:S(2)}) %collective-permute-start.1) | collective-permute-done | bytes 524320 | tf_op jit(solution)/shard_map/while/body/ppermute | solution.py:24
  228.1 7.5 %all-to-all-start = ((f32[16,1,12]{2,1,0:T(1,128)}), f32[16,1,12]{2,1,0:T(1,128)S(1)}, u32[]{:S(2)}, u32[]{:S(2)}) async-start(f32[16,1,12]{2,1,0:T(1,128)} %broadcast_in_dim.42), calls=%async_computation | async-start | bytes 16384 | tf_op jit(solution)/shard_map/while/body/all_to_all | solution.py:33
  235.6 6.4 %all-to-all-done = f32[16,1,12]{2,1,0:T(1,128)S(1)} async-done(((f32[16,1,12]{2,1,0:T(1,128)}), f32[16,1,12]{2,1,0:T(1,128)S(1)}, u32[]{:S(2)}, u32[]{:S(2)}) %all-to-all-start) | async-done | bytes 800 | tf_op jit(solution)/shard_map/while/body/all_to_all | solution.py:33
  249.5 4.7 %collective-permute-done = f32[4,2,1,128,128]{4,3,2,0,1:T(8,128)S(1)} collective-permute-done((f32[4,2,1,128,128]{4,3,2,0,1:T(8,128)S(1)}, f32[4,2,1,128,128]{4,3,2,0,1:T(8,128)S(1)}, u32[]{:S(2)}, u32[]{:S(2)}) %collective-permute-start) | collective-permute-done | bytes 524320 | tf_op jit(solution)/shard_map/while/body/ppermute | solution.py:22
  254.2 3.8 %collective-permute-done.1 = f32[4,2,1,128,128]{4,3,2,0,1:T(8,128)S(1)} collective-permute-done((f32[4,2,1,128,128]{4,3,2,0,1:T(8,128)S(1)}, f32[4,2,1,128,128]{4,3,2,0,1:T(8,128)S(1)}, u32[]{:S(2)}, u32[]{:S(2)}) %collective-permute-start.1) | collective-permute-done | bytes 524320 | tf_op jit(solution)/shard_map/while/body/ppermute | solution.py:24
  260.0 7.5 %all-to-all-start = ((f32[16,1,12]{2,1,0:T(1,128)}), f32[16,1,12]{2,1,0:T(1,128)S(1)}, u32[]{:S(2)}, u32[]{:S(2)}) async-start(f32[16,1,12]{2,1,0:T(1,128)} %broadcast_in_dim.42), calls=%async_computation | async-start | bytes 16384 | tf_op jit(solution)/shard_map/while/body/all_to_all | solution.py:33
  267.5 6.4 %all-to-all-done = f32[16,1,12]{2,1,0:T(1,128)S(1)} async-done(((f32[16,1,12]{2,1,0:T(1,128)}), f32[16,1,12]{2,1,0:T(1,128)S(1)}, u32[]{:S(2)}, u32[]{:S(2)}) %all-to-all-start) | async-done | bytes 800 | tf_op jit(solution)/shard_map/while/body/all_to_all | solution.py:33
  281.0 17.8 %all-to-all-start.3 = ((f32[4,2,2,128,128]{4,2,0,1,3:T(2,128)}), f32[4,2,2,128,128]{4,2,0,1,3:T(2,128)S(1)}, u32[]{:S(2)}, u32[]{:S(2)}) async-start(f32[4,2,2,128,128]{4,2,0,1,3:T(2,128)} %pad_maximum_fusion.6), calls=%async_computation.3 | async-start | bytes 2097152 | tf_op jit(solution)/shard_map/all_to_all | solution.py:140
  298.9 28.0 %all-to-all-done.3 = f32[4,2,2,128,128]{4,2,0,1,3:T(2,128)S(1)} async-done(((f32[4,2,2,128,128]{4,2,0,1,3:T(2,128)}), f32[4,2,2,128,128]{4,2,0,1,3:T(2,128)S(1)}, u32[]{:S(2)}, u32[]{:S(2)}) %all-to-all-start.3) | async-done | bytes 1048608 | tf_op jit(solution)/shard_map/all_to_all | solution.py:140
  328.9 20.4 %all_to_all.72 = f32[64,2,8,128]{3,2,1,0:T(8,128)S(1)} all-to-all(f32[64,2,8,128]{3,2,1,0:T(8,128)S(1)} %copy.60), channel_id=1, replica_groups=mesh['tm'=16,'space'=16] {'tm'}, dimensions={0} | all-to-all | bytes 1048576 | tf_op jit(solution)/shard_map/all_to_all | solution.py:148
  (116 shorter events, 73.2 us)
Async XLA Ops:
  40.4 3.9 %copy-start = (s32[64]{0:T(128)S(1)}, s32[64]{0:T(128)}, u32[]{:S(2)}) copy-start(s32[64]{0:T(128)} %param.7) | copy-start | bytes 772
  40.4 31.1 %all-to-all-start.2 = ((f32[16,4,2,2,8,128]{5,1,4,3,2,0:T(4,128)}), f32[16,4,2,2,8,128]{5,1,4,3,2,0:T(4,128)S(1)}, u32[]{:S(2)}, u32[]{:S(2)}) async-start(f32[16,4,2,2,8,128]{5,1,4,3,2,0:T(4,128)} %fusion.38), calls=%async_computation.2 | async-start | bytes 2097152 | tf_op jit(solution)/shard_map/all_to_all | solution.py:137
  71.6 1.7 copy-start.1
  74.4 14.0 %collective-permute-start = (f32[4,2,1,128,128]{4,3,2,0,1:T(8,128)S(1)}, f32[4,2,1,128,128]{4,3,2,0,1:T(8,128)S(1)}, u32[]{:S(2)}, u32[]{:S(2)}) collective-permute-start(f32[4,2,1,128,128]{4,3,2,0,1:T(8,128)S(1)} %get-tuple-element.368), channel_id=1, source_target_pairs={{0,1},{1,2},{2,3},{3,4},{4,5},{5,6},{6,7},{7,8},{8,9},{9,10},{10,1... | collective-permute-start | bytes 1572872 | tf_op jit(solution)/shard_map/while/body/ppermute | solution.py:22
  77.5 15.0 %collective-permute-start.1 = (f32[4,2,1,128,128]{4,3,2,0,1:T(8,128)S(1)}, f32[4,2,1,128,128]{4,3,2,0,1:T(8,128)S(1)}, u32[]{:S(2)}, u32[]{:S(2)}) collective-permute-start(f32[4,2,1,128,128]{4,3,2,0,1:T(8,128)S(1)} %get-tuple-element.369), channel_id=1, source_target_pairs={{1,0},{2,1},{3,2},{4,3},{5,4},{6,5},{7,6},{8,7},{9,8},{10,9},{11,1... | collective-permute-start | bytes 1572872 | tf_op jit(solution)/shard_map/while/body/ppermute | solution.py:24
  94.5 14.7 %all-to-all-start = ((f32[16,1,12]{2,1,0:T(1,128)}), f32[16,1,12]{2,1,0:T(1,128)S(1)}, u32[]{:S(2)}, u32[]{:S(2)}) async-start(f32[16,1,12]{2,1,0:T(1,128)} %broadcast_in_dim.42), calls=%async_computation | async-start | bytes 16384 | tf_op jit(solution)/shard_map/while/body/all_to_all | solution.py:33
  113.2 11.6 %collective-permute-start = (f32[4,2,1,128,128]{4,3,2,0,1:T(8,128)S(1)}, f32[4,2,1,128,128]{4,3,2,0,1:T(8,128)S(1)}, u32[]{:S(2)}, u32[]{:S(2)}) collective-permute-start(f32[4,2,1,128,128]{4,3,2,0,1:T(8,128)S(1)} %get-tuple-element.368), channel_id=1, source_target_pairs={{0,1},{1,2},{2,3},{3,4},{4,5},{5,6},{6,7},{7,8},{8,9},{9,10},{10,1... | collective-permute-start | bytes 1572872 | tf_op jit(solution)/shard_map/while/body/ppermute | solution.py:22
  115.3 13.4 %collective-permute-start.1 = (f32[4,2,1,128,128]{4,3,2,0,1:T(8,128)S(1)}, f32[4,2,1,128,128]{4,3,2,0,1:T(8,128)S(1)}, u32[]{:S(2)}, u32[]{:S(2)}) collective-permute-start(f32[4,2,1,128,128]{4,3,2,0,1:T(8,128)S(1)} %get-tuple-element.369), channel_id=1, source_target_pairs={{1,0},{2,1},{3,2},{4,3},{5,4},{6,5},{7,6},{8,7},{9,8},{10,9},{11,1... | collective-permute-start | bytes 1572872 | tf_op jit(solution)/shard_map/while/body/ppermute | solution.py:24
  130.7 14.3 %all-to-all-start = ((f32[16,1,12]{2,1,0:T(1,128)}), f32[16,1,12]{2,1,0:T(1,128)S(1)}, u32[]{:S(2)}, u32[]{:S(2)}) async-start(f32[16,1,12]{2,1,0:T(1,128)} %broadcast_in_dim.42), calls=%async_computation | async-start | bytes 16384 | tf_op jit(solution)/shard_map/while/body/all_to_all | solution.py:33
  148.9 9.2 %collective-permute-start = (f32[4,2,1,128,128]{4,3,2,0,1:T(8,128)S(1)}, f32[4,2,1,128,128]{4,3,2,0,1:T(8,128)S(1)}, u32[]{:S(2)}, u32[]{:S(2)}) collective-permute-start(f32[4,2,1,128,128]{4,3,2,0,1:T(8,128)S(1)} %get-tuple-element.368), channel_id=1, source_target_pairs={{0,1},{1,2},{2,3},{3,4},{4,5},{5,6},{6,7},{7,8},{8,9},{9,10},{10,1... | collective-permute-start | bytes 1572872 | tf_op jit(solution)/shard_map/while/body/ppermute | solution.py:22
  151.0 11.0 %collective-permute-start.1 = (f32[4,2,1,128,128]{4,3,2,0,1:T(8,128)S(1)}, f32[4,2,1,128,128]{4,3,2,0,1:T(8,128)S(1)}, u32[]{:S(2)}, u32[]{:S(2)}) collective-permute-start(f32[4,2,1,128,128]{4,3,2,0,1:T(8,128)S(1)} %get-tuple-element.369), channel_id=1, source_target_pairs={{1,0},{2,1},{3,2},{4,3},{5,4},{6,5},{7,6},{8,7},{9,8},{10,9},{11,1... | collective-permute-start | bytes 1572872 | tf_op jit(solution)/shard_map/while/body/ppermute | solution.py:24
  164.0 14.3 %all-to-all-start = ((f32[16,1,12]{2,1,0:T(1,128)}), f32[16,1,12]{2,1,0:T(1,128)S(1)}, u32[]{:S(2)}, u32[]{:S(2)}) async-start(f32[16,1,12]{2,1,0:T(1,128)} %broadcast_in_dim.42), calls=%async_computation | async-start | bytes 16384 | tf_op jit(solution)/shard_map/while/body/all_to_all | solution.py:33
  182.2 8.2 %collective-permute-start = (f32[4,2,1,128,128]{4,3,2,0,1:T(8,128)S(1)}, f32[4,2,1,128,128]{4,3,2,0,1:T(8,128)S(1)}, u32[]{:S(2)}, u32[]{:S(2)}) collective-permute-start(f32[4,2,1,128,128]{4,3,2,0,1:T(8,128)S(1)} %get-tuple-element.368), channel_id=1, source_target_pairs={{0,1},{1,2},{2,3},{3,4},{4,5},{5,6},{6,7},{7,8},{8,9},{9,10},{10,1... | collective-permute-start | bytes 1572872 | tf_op jit(solution)/shard_map/while/body/ppermute | solution.py:22
  184.3 9.9 %collective-permute-start.1 = (f32[4,2,1,128,128]{4,3,2,0,1:T(8,128)S(1)}, f32[4,2,1,128,128]{4,3,2,0,1:T(8,128)S(1)}, u32[]{:S(2)}, u32[]{:S(2)}) collective-permute-start(f32[4,2,1,128,128]{4,3,2,0,1:T(8,128)S(1)} %get-tuple-element.369), channel_id=1, source_target_pairs={{1,0},{2,1},{3,2},{4,3},{5,4},{6,5},{7,6},{8,7},{9,8},{10,9},{11,1... | collective-permute-start | bytes 1572872 | tf_op jit(solution)/shard_map/while/body/ppermute | solution.py:24
  196.2 14.0 %all-to-all-start = ((f32[16,1,12]{2,1,0:T(1,128)}), f32[16,1,12]{2,1,0:T(1,128)S(1)}, u32[]{:S(2)}, u32[]{:S(2)}) async-start(f32[16,1,12]{2,1,0:T(1,128)} %broadcast_in_dim.42), calls=%async_computation | async-start | bytes 16384 | tf_op jit(solution)/shard_map/while/body/all_to_all | solution.py:33
  214.1 8.2 %collective-permute-start = (f32[4,2,1,128,128]{4,3,2,0,1:T(8,128)S(1)}, f32[4,2,1,128,128]{4,3,2,0,1:T(8,128)S(1)}, u32[]{:S(2)}, u32[]{:S(2)}) collective-permute-start(f32[4,2,1,128,128]{4,3,2,0,1:T(8,128)S(1)} %get-tuple-element.368), channel_id=1, source_target_pairs={{0,1},{1,2},{2,3},{3,4},{4,5},{5,6},{6,7},{7,8},{8,9},{9,10},{10,1... | collective-permute-start | bytes 1572872 | tf_op jit(solution)/shard_map/while/body/ppermute | solution.py:22
  216.2 9.9 %collective-permute-start.1 = (f32[4,2,1,128,128]{4,3,2,0,1:T(8,128)S(1)}, f32[4,2,1,128,128]{4,3,2,0,1:T(8,128)S(1)}, u32[]{:S(2)}, u32[]{:S(2)}) collective-permute-start(f32[4,2,1,128,128]{4,3,2,0,1:T(8,128)S(1)} %get-tuple-element.369), channel_id=1, source_target_pairs={{1,0},{2,1},{3,2},{4,3},{5,4},{6,5},{7,6},{8,7},{9,8},{10,9},{11,1... | collective-permute-start | bytes 1572872 | tf_op jit(solution)/shard_map/while/body/ppermute | solution.py:24
  228.1 14.0 %all-to-all-start = ((f32[16,1,12]{2,1,0:T(1,128)}), f32[16,1,12]{2,1,0:T(1,128)S(1)}, u32[]{:S(2)}, u32[]{:S(2)}) async-start(f32[16,1,12]{2,1,0:T(1,128)} %broadcast_in_dim.42), calls=%async_computation | async-start | bytes 16384 | tf_op jit(solution)/shard_map/while/body/all_to_all | solution.py:33
  246.0 8.2 %collective-permute-start = (f32[4,2,1,128,128]{4,3,2,0,1:T(8,128)S(1)}, f32[4,2,1,128,128]{4,3,2,0,1:T(8,128)S(1)}, u32[]{:S(2)}, u32[]{:S(2)}) collective-permute-start(f32[4,2,1,128,128]{4,3,2,0,1:T(8,128)S(1)} %get-tuple-element.368), channel_id=1, source_target_pairs={{0,1},{1,2},{2,3},{3,4},{4,5},{5,6},{6,7},{7,8},{8,9},{9,10},{10,1... | collective-permute-start | bytes 1572872 | tf_op jit(solution)/shard_map/while/body/ppermute | solution.py:22
  248.1 9.9 %collective-permute-start.1 = (f32[4,2,1,128,128]{4,3,2,0,1:T(8,128)S(1)}, f32[4,2,1,128,128]{4,3,2,0,1:T(8,128)S(1)}, u32[]{:S(2)}, u32[]{:S(2)}) collective-permute-start(f32[4,2,1,128,128]{4,3,2,0,1:T(8,128)S(1)} %get-tuple-element.369), channel_id=1, source_target_pairs={{1,0},{2,1},{3,2},{4,3},{5,4},{6,5},{7,6},{8,7},{9,8},{10,9},{11,1... | collective-permute-start | bytes 1572872 | tf_op jit(solution)/shard_map/while/body/ppermute | solution.py:24
  260.0 14.0 %all-to-all-start = ((f32[16,1,12]{2,1,0:T(1,128)}), f32[16,1,12]{2,1,0:T(1,128)S(1)}, u32[]{:S(2)}, u32[]{:S(2)}) async-start(f32[16,1,12]{2,1,0:T(1,128)} %broadcast_in_dim.42), calls=%async_computation | async-start | bytes 16384 | tf_op jit(solution)/shard_map/while/body/all_to_all | solution.py:33
  281.0 45.9 %all-to-all-start.3 = ((f32[4,2,2,128,128]{4,2,0,1,3:T(2,128)}), f32[4,2,2,128,128]{4,2,0,1,3:T(2,128)S(1)}, u32[]{:S(2)}, u32[]{:S(2)}) async-start(f32[4,2,2,128,128]{4,2,0,1,3:T(2,128)} %pad_maximum_fusion.6), calls=%async_computation.3 | async-start | bytes 2097152 | tf_op jit(solution)/shard_map/all_to_all | solution.py:140
